TPU v7x, 128 devices: a whole 4x4x4 slice. The times are simulated.
128 devices in a mesh: grp: 2 (over x_lo), dp: 64 (over y, x_hi, z, core).
Axes of the slice: x: 4 (x_hi: 2, x_lo: 2; x = x_hi * 2 + x_lo), y: 4, z: 4, core: 2. Of those that a mesh axis runs over, the one named last changes fastest.
Arguments:
- teacher_in: bfloat16 [32768, 1664], P('dp'), may hold values from -6 to 6
- teacher_gain: float32 [1664], replicated, may hold values from 0.5 to 1.5
- teacher_up: bfloat16 [1664, 4096], P('dp', 'grp'), may hold values from -0.15625 to 0.15625
- teacher_down: bfloat16 [1664, 4096], P('dp', 'grp'), may hold values from -0.09375 to 0.09375
- student_in: bfloat16 [32768, 768], P('dp'), may hold values from -6 to 6
- student_gain: float32 [768], replicated, may hold values from 0.5 to 1.5
- student_up: bfloat16 [768, 1536], P(None, ('grp', 'dp')), may hold values from -0.21875 to 0.21875
- student_down: bfloat16 [1536, 768], P(('grp', 'dp')), may hold values from -0.15625 to 0.15625
- student_head: bfloat16 [768, 1664], P(None, ('grp', 'dp')), may hold values from -0.21875 to 0.21875
- student_proj: bfloat16 [768, 512], P(None, ('grp', 'dp')), may hold values from -1 to 1
- word_table: bfloat16 [49408, 512], P(('grp', 'dp')), may hold values from -6 to 6
- caption_ids: int32 [128, 77], replicated, may hold values from 0 to 49407
- positive: int32 [128], replicated, may hold values from 0 to 127, each once
Outputs:
- loss: float32 [], replicated
- grad_up: float32 [768, 1536], P(None, ('grp', 'dp'))
- grad_down: float32 [1536, 768], P(('grp', 'dp'))
- grad_head: float32 [768, 1664], P(None, ('grp', 'dp'))
- grad_proj: float32 [768, 512], P(None, ('grp', 'dp'))
Inputs may be any that keep to these rules, and one draw needn't show every extreme that they name: Each caption is the positive of exactly one image.
All inputs are finite; a program needn't handle non-finite values.
Results may differ from a plain program's by a relative error of at most 0.0065.
Values may be sent and summed in bfloat16 or wider, within the bound.
A program may use at most 128 MiB of HBM per device.

v0:
```python
import jax
import jax.numpy as jnp
from jax import lax
from jax.experimental import pallas as pl
from jax.experimental.pallas import tpu as pltpu
from jax.sharding import PartitionSpec as P

CAP_LEN = 77
PATCHES = 256
BLK = 16
MESH = pl.DeviceIdType.MESH
VM = pl.BlockSpec(memory_space=pltpu.VMEM)


def coords():
    grp = lax.axis_index("grp")
    dp = lax.axis_index("dp")
    x_hi = (dp // 8) % 2
    return {
        "x": 2 * x_hi + grp,
        "y": dp // 16,
        "z": (dp // 2) % 4,
        "core": dp % 2,
    }


def device(at):
    return (at["x"] % 2, at["y"] * 16 + (at["x"] // 2) * 8 + at["z"] * 2 + at["core"])


def shifted(me, axis, step):
    if axis == "core":
        return {**me, "core": 1 - me["core"]}
    return {**me, axis: (me[axis] + step) % 4}


def enter(me, axes=("x", "y", "z"), steps=(1, 2, 3)):
    barrier = pltpu.get_barrier_semaphore()
    peers = [shifted(me, "core", 1)]
    for axis in axes:
        for step in steps:
            peers.append(shifted(me, axis, step))
    for peer in peers:
        pl.semaphore_signal(barrier, inc=1, device_id=device(peer), device_id_type=MESH)
    pl.semaphore_wait(barrier, len(peers))


class Copies:
    def __init__(self, send, recv):
        self.send, self.recv, self.count, self.open = send, recv, 0, []

    def start(self, src, dst, peer):
        copy = pltpu.make_async_remote_copy(
            src_ref=src,
            dst_ref=dst,
            send_sem=self.send.at[self.count],
            recv_sem=self.recv.at[self.count],
            device_id=device(peer),
            device_id_type=MESH,
        )
        self.count += 1
        copy.start()
        self.open.append(copy)
        return copy

    def finish(self):
        for copy in self.open:
            copy.wait_send()


def pick(ref, at, tail=()):
    x = at.get("x")
    whole = slice(None)
    index = (
        whole if x is None else x % 2,
        at.get("y", whole),
        whole if x is None else x // 2,
        at.get("z", whole),
    )
    if "core" in at:
        index += (at["core"],)
    return ref.at[index + tail]


def half(ref, side):
    if len(ref.shape) > 2:
        size = ref.shape[0] // 2
        return ref.at[pl.ds(side * size, size)]
    lanes = ref.shape[1] // 128
    cut = lanes // 2 * 128
    if side == 0:
        return ref.at[:, pl.ds(0, cut)]
    return ref.at[:, pl.ds(cut, ref.shape[1] - cut)]


def pick_teacher(ref, at, tail=()):
    whole = slice(None)
    index = (
        at.get("y", whole),
        at["x"] // 2,
        at.get("z", whole),
        at["core"],
    )
    return ref.at[index + tail]


def ring(copies, me, sibling, view, order, held, pushes):
    for axis in order:
        up, down, far = (shifted(me, axis, s) for s in (1, 3, 2))
        block = view(held)
        right = copies.start(block, block, up)
        left = copies.start(block, block, down)
        yield
        right.wait_recv()
        from_down = view({**held, axis: down[axis]})
        right2 = copies.start(half(from_down, 0), half(from_down, 0), up)
        pushes.append(copies.start(from_down, from_down, sibling))
        left.wait_recv()
        from_up = view({**held, axis: up[axis]})
        left2 = copies.start(half(from_up, 1), half(from_up, 1), down)
        pushes.append(copies.start(from_up, from_up, sibling))
        yield
        right2.wait_recv()
        left2.wait_recv()
        from_far = view({**held, axis: far[axis]})
        pushes.append(copies.start(from_far, from_far, sibling))
        held.pop(axis)


def student_chain(copies, me, sibling, ref, order):
    view = lambda at: pick(ref, at)
    own = view(me)
    pushes = [copies.start(own, own, sibling)]
    yield from ring(copies, me, sibling, view, order, dict(me), pushes)
    yield
    for copy in pushes:
        copy.wait_recv()


def teacher_chain(copies, me, sibling, ref, part, order, other):
    tail = (pl.ds(part * BLK, BLK),)
    view = lambda at: pick_teacher(ref, at, tail)
    pushes = []
    held = dict(me)
    if other:
        far = shifted(me, "x", 2)
        copy = copies.start(view(me), view(me), far)
        yield
        copy.wait_recv()
        held = dict(far)
    block = view(held)
    pushes.append(copies.start(block, block, sibling))
    yield from ring(copies, me, sibling, view, order, held, pushes)
    yield
    for copy in pushes:
        copy.wait_recv()


def caption_chain(copies, me, sibling, p_ref, out_ref, other, at_x, at_y, at_z):
    copy = copies.start(p_ref, other, sibling)
    yield
    copy.wait_recv()
    other[...] = other[...] + p_ref[...]

    def exchange(axis, source, slots):
        waits = []
        for step in (2, 1, 3):
            peer = shifted(me, axis, step)
            waits.append(copies.start(source.at[peer[axis]], slots.at[me[axis]], peer))
        slots[me[axis]] = source[me[axis]]
        return waits

    def total(waits, slots):
        for copy in waits:
            copy.wait_recv()
        return (slots[0] + slots[1]) + (slots[2] + slots[3])

    def spread(axis, view):
        return [copies.start(view, view, shifted(me, axis, step)) for step in (2, 1, 3)]

    waits = exchange("x", other, at_x)
    yield
    at_x[4] = total(waits, at_x)
    waits = exchange("y", at_x.at[4], at_y)
    yield
    at_y[4] = total(waits, at_y)
    waits = exchange("z", at_y.at[4], at_z)
    yield
    own = out_ref.at[me["x"], me["y"], me["z"]]
    own[...] = total(waits, at_z)
    for axis, view in (
        ("z", own),
        ("y", out_ref.at[me["x"], me["y"]]),
        ("x", out_ref.at[me["x"]]),
    ):
        waits = spread(axis, view)
        yield
        for copy in waits:
            copy.wait_recv()


def rows_padded(values, rows):
    short = rows - values.shape[0]
    if short == 0:
        return values
    return jnp.concatenate([values, jnp.zeros((short, values.shape[1]), values.dtype)], 0)


def image_chain(copies, me, out):
    held = dict(me)
    for axis in ("core", "x", "z", "y"):
        view = pick(out, held)
        steps = (1,) if axis == "core" else (2, 1, 3)
        waits = [copies.start(view, view, shifted(me, axis, step)) for step in steps]
        yield
        for copy in waits:
            copy.wait_recv()
        held.pop(axis)


def norm_rows(values, gain):
    center = values - jnp.mean(values, -1, keepdims=True)
    variance = jnp.mean(center * center, -1, keepdims=True)
    return (center * lax.rsqrt(variance + 1e-05) * gain).astype(jnp.bfloat16)


ORDERS = (("x", "y", "z"), ("y", "z", "x"), ("z", "x", "y"))
COLS = 256


def dims_of(axes):
    dims = []
    if "x" in axes:
        dims.append(2)
    if "y" in axes:
        dims.append(4)
    if "x" in axes:
        dims.append(2)
    if "z" in axes:
        dims.append(4)
    return tuple(dims)


def rest_of(order, phase):
    return [a for a in ("x", "y", "z") if a not in order[: phase + 1]]


def half_shape(order, phase, rows):
    shape = dims_of(rest_of(order, phase)) + (rows, COLS)
    if len(shape) == 2:
        return (rows, COLS // 2)
    return (shape[0] // 2,) + shape[1:]


def add_into(dst, srcs):
    lead = dst.shape[:-2]
    total = 1
    for size in lead:
        total *= size

    def one(index):
        value = dst[index].astype(jnp.float32)
        for src in srcs:
            value = value + src[index].astype(jnp.float32)
        dst[index] = value.astype(dst.dtype)

    if total == 1:
        one((0,) * len(lead) + (slice(None), slice(None)))
        return

    def body(n, carry):
        index = []
        rest = n
        for size in reversed(lead):
            index.append(rest % size)
            rest = rest // size
        one(tuple(reversed(index)))
        return carry

    lax.fori_loop(0, total, body, 0)


def rows_of(view, first, count, cols=None):
    lead = (slice(None),) * (len(view.shape) - 2)
    return view.at[lead + (pl.ds(first, count), slice(None) if cols is None else cols)]


class Scatter:
    def __init__(self, copies, me, sibling, pack, head, accs, hold):
        self.copies, self.me, self.sibling = copies, me, sibling
        self.pack, self.head, self.accs, self.hold = pack, head, accs, hold
        self.opening = {}

    def first(self, t, phase):
        return self.hold[(t * 3 + phase) * 2]

    def second(self, t, phase):
        return self.hold[(t * 3 + phase) * 2 + 1]

    def source(self, which, t, at):
        ref = self.head if which else self.pack
        return rows_of(pick(ref, at), 0, ref.shape[-2], pl.ds(t * COLS, COLS))

    def place(self, which, t, at):
        n_pack = self.pack.shape[-2]
        first, count = (n_pack, self.head.shape[-2]) if which else (0, n_pack)
        return rows_of(pick(self.accs[t], at), first, count)

    def at(self, t, step):
        axis = ORDERS[t][0]
        return {axis: shifted(self.me, axis, step)[axis]}

    def push(self, which):
        for step in (2, 1, 3, 0):
            for t in range(3):
                at = self.at(t, step)
                self.opening[which, t, step] = self.copies.start(
                    self.source(which, t, {**at, "core": self.sibling["core"]}),
                    self.place(which, t, at),
                    self.sibling,
                )

    def opened(self, t, step):
        at = self.at(t, step)
        for which in range(2):
            self.opening[which, t, step].wait_recv()
            add_into(
                self.place(which, t, at),
                [self.source(which, t, {**at, "core": self.me["core"]})],
            )

    def open_phase(self, t, phase, held):
        axis = ORDERS[t][phase]
        far = shifted(self.me, axis, 2)
        view = pick(self.accs[t], {**held, axis: far[axis]})
        up, down = shifted(self.me, axis, 1), shifted(self.me, axis, 3)
        return (
            self.copies.start(half(view, 0), self.first(t, phase).at[0], up),
            self.copies.start(half(view, 1), self.first(t, phase).at[1], down),
        )

    def finish(self, s_ref, s_slots, o_up, o_down, o_head):
        copies, me, accs = self.copies, self.me, self.accs
        n_pack = self.pack.shape[-2]
        s_wait = [copies.start(s_ref, s_slots.at[0, me["core"]], self.sibling)]
        s_slots[0, me["core"]] = s_ref[...]
        pending = [None] * 3
        held = [dict() for _ in range(3)]
        for t in range(3):
            self.opened(t, 2)
            pending[t] = self.open_phase(t, 0, held[t])
        for step in (1, 3, 0):
            for t in range(3):
                self.opened(t, step)
        for copy in s_wait:
            copy.wait_recv()
        s_value = s_slots[0, 0] + s_slots[0, 1]
        for phase in range(3):
            s_axis = ("x", "y", "z")[phase]
            s_slots[phase + 1, me[s_axis]] = s_value
            s_wait = []
            for step in (1, 2, 3):
                s_mine = s_slots.at[phase + 1, me[s_axis]]
                s_wait.append(copies.start(s_mine, s_mine, shifted(me, s_axis, step)))
            for t in range(3):
                axis = ORDERS[t][phase]
                up, down = shifted(me, axis, 1), shifted(me, axis, 3)
                to_up = pick(accs[t], {**held[t], axis: up[axis]})
                to_down = pick(accs[t], {**held[t], axis: down[axis]})
                pending[t][0].wait_recv()
                add_into(half(to_up, 0), [self.first(t, phase).at[0]])
                a = copies.start(to_up, self.second(t, phase).at[0], up)
                pending[t][1].wait_recv()
                add_into(half(to_down, 1), [self.first(t, phase).at[1]])
                b = copies.start(to_down, self.second(t, phase).at[1], down)
                pending[t] = (a, b)
            for t in range(3):
                axis = ORDERS[t][phase]
                pending[t][0].wait_recv()
                pending[t][1].wait_recv()
                held[t][axis] = me[axis]
                mine = pick(accs[t], held[t])
                got = self.second(t, phase)
                if phase < 2:
                    add_into(mine, [got.at[0], got.at[1]])
                    pending[t] = self.open_phase(t, phase + 1, held[t])
                else:
                    value = mine[...].astype(jnp.float32) + got[0].astype(jnp.float32)
                    value = value + got[1].astype(jnp.float32)
                    cols = pl.ds(t * COLS, COLS)
                    hid = o_up.shape[0]
                    o_up[:, cols] = value[:hid]
                    o_down[:, cols] = value[hid:n_pack]
                    o_head[:, cols] = value[n_pack : n_pack + o_head.shape[0]]
            for copy in s_wait:
                copy.wait_recv()
            s_value = (s_slots[phase + 1, 0] + s_slots[phase + 1, 1]) + (
                s_slots[phase + 1, 2] + s_slots[phase + 1, 3]
            )
        return s_value


def gelu_tanh(values):
    return jax.nn.gelu(values, approximate=True)


def dot(a, b, da, db):
    return lax.dot_general(a, b, (((da,), (db,)), ((), ())), preferred_element_type=jnp.float32)


def exact(a, b, da, db):
    return lax.dot_general(
        a, b, (((da,), (db,)), ((), ())),
        precision=lax.Precision.HIGHEST, preferred_element_type=jnp.float32,
    )


ORDER = (
    "PHQuKUvVDdnnPHKQnuUnPHQvdDnKuUeEVHQPveEuKUVPvEeuUVDdeKuUvEV",
    "PHQdDePKEvVPssdssvsVssKDsSIehdhhIHDEehhhhhE",
)


def step_kernel(
    t_up, t_down, up, down, head, proj, words, t_in, t_gain, s_in, s_gain, target_of,
    o_up, o_down, o_head, o_proj, o_loss,
    g_up, g_down, g_pack, g_head, g_proj, captions, images, gates, acts, normed, rounded, wide,
    far, near, got, t_normed, t_act, s_acc, grad_out, grad_img, d_pack, d_head, f_tile,
    other, at_x, at_y, at_z, s_slots, send, recv, *stores
):
    accs, hold = stores[:3], stores[3:]
    me = coords()
    grp = me["x"] % 2
    shard = grp * 64 + me["y"] * 16 + me["x"] // 2 * 8 + me["z"] * 2 + me["core"]
    sibling = shifted(me, "core", 1)
    feat, hid = head.shape[0], up.shape[0]
    width = t_in.shape[1]
    f32, bf16 = jnp.float32, jnp.bfloat16
    iota = lambda shape, axis: lax.broadcasted_iota(jnp.int32, shape, axis)

    pick(g_pack, me)[...] = jnp.concatenate([up[...].astype(f32), down[...].astype(f32)], 0).astype(
        bf16
    )
    pick(g_head, me)[...] = rows_padded(head[...].astype(f32), BLK).astype(bf16)
    values = proj[...].astype(f32)
    cut = values.shape[1] // 2
    pick(g_proj, me)[...] = jnp.concatenate([values[:, :cut], values[:, cut:]], 0).astype(bf16)
    for source, out in ((t_up, g_up), (t_down, g_down)):
        values = source[...].astype(f32)
        for part in range(2):
            cut = values[part * feat : (part + 1) * feat]
            pick_teacher(out, me, (pl.ds(part * BLK, BLK),))[...] = rows_padded(cut, BLK).astype(
                bf16
            )
    enter(me)
    copies = Copies(send, recv)

    def teacher(ref, part, other_x):
        order = ("y", "z") if part == 0 else ("z", "y")
        return teacher_chain(copies, me, sibling, ref, part, order, other_x)

    chains = {
        "P": student_chain(copies, me, sibling, g_pack, ("y", "z", "x")),
        "H": student_chain(copies, me, sibling, g_head, ("z", "y", "x")),
        "Q": student_chain(copies, me, sibling, g_proj, ("z", "y", "x")),
        "K": caption_chain(copies, me, sibling, words, captions, other, at_x, at_y, at_z),
        "I": image_chain(copies, me, images),
    }
    for part in range(2):
        chains["uU"[part]] = teacher(g_up, part, False)
        chains["vV"[part]] = teacher(g_up, part, True)
        chains["dD"[part]] = teacher(g_down, part, False)
        chains["eE"[part]] = teacher(g_down, part, True)

    own_rows = gates.shape[0]
    own = pl.ds(pl.multiple_of(grp * own_rows, own_rows), own_rows)
    partner_rows = pl.ds(pl.multiple_of((1 - grp) * own_rows, own_rows), own_rows)
    step = 256
    span = step // BLK * feat

    def student_norm():
        normed[...] = norm_rows(s_in[own, :].astype(f32), s_gain[...])

    def teacher_norm():
        def body(r, carry):
            rows = pl.ds(pl.multiple_of(r * 64, 64), 64)
            t_act[rows, pl.ds(0, width)] = norm_rows(t_in[rows, :].astype(f32), t_gain[...])
            return carry

        lax.fori_loop(0, t_in.shape[0] // 64, body, 0)

    def spread(j):
        base = span * j // 128 * 128
        size = -(-(span * j + span - base) // 128) * 128
        row = iota((size, step), 0) + base
        col = iota((size, step), 1)
        place = span * j + col // BLK * feat + col % BLK
        chosen = jnp.where((row == place) & (col % BLK < feat), 1.0, 0.0).astype(bf16)
        window = pl.ds(base, size)
        cols = pl.ds(j * step, step)
        t_normed[:, cols] = dot(t_act[:, window], chosen, 1, 0).astype(bf16)
        wide[:, cols] = dot(t_in[own, window], chosen, 1, 0).astype(bf16)

    def hidden(j):
        cols = pl.ds(j * step, step)
        weights = g_up[:, :, :, :, :, cols].reshape(-1, step)
        t_act[:, cols] = gelu_tanh(dot(t_normed[...], weights, 1, 0)).astype(bf16)

    def branch(y, rows, out):
        weights = g_down[y].reshape(-1, g_down.shape[-1])
        out[y] = dot(t_act[rows, :], weights, 1, 1).astype(bf16)

    def ups(shape):
        return iota(shape, 1) % (2 * hid) < hid

    def student(n):
        weights = g_pack[n // 4, n % 4].reshape(-1, g_pack.shape[-1])
        size = weights.shape[0]
        cols = pl.ds(n * size, size)
        gate = dot(normed[...], weights, 1, 1)
        gates[:, cols] = gate
        act = jnp.where(ups(gate.shape), gelu_tanh(gate), 0.0)
        act = pltpu.roll(act, hid, 1).astype(bf16)
        acts[:, cols] = act
        part = dot(act, weights, 1, 0)
        s_acc[...] = part + (s_in[own, :].astype(f32) if n == 0 else s_acc[...])

    def student_end():
        value = s_acc[...]
        rounded[...] = value.astype(bf16)
        pooled = jnp.sum(value, 0, keepdims=True) / PATCHES
        lanes = [pooled[:, i * 128 : (i + 1) * 128] for i in range(pooled.shape[1] // 128)]
        tile = rows_padded(jnp.concatenate(lanes, 0), 8)
        pick(images, me)[...] = tile.astype(bf16).astype(f32)

    work = {
        "n": [student_norm, teacher_norm]
        + [lambda k=k: [spread(j) for j in range(k, k + 3) if j < 8] for k in (0, 3, 6)],
        "h": [lambda j=j: hidden(j) for j in range(8)],
        "s": [lambda n=n: student(n) for n in range(8)],
        "S": [student_end],
    }
    for line in ORDER:
        for name in line:
            if name in work:
                work[name].pop(0)()
            else:
                next(chains[name], None)

    partner = {**me, "x": me["x"] + 1 - 2 * grp}
    exchange = []
    for y in range(4):
        branch(y, partner_rows, far)
        exchange.append(copies.start(far.at[y], got.at[y], partner))
    next(chains["I"], None)
    branch(0, own, near)
    branch(1, own, near)
    next(chains["I"], None)
    branch(2, own, near)
    branch(3, own, near)
    for turn in range(8):
        for one in chains.values():
            next(one, None)

    n_img = 128
    cols_dev = o_proj.shape[0]
    flat = images.reshape(n_img * 8, 128)
    pooled = [flat[pl.ds(i, n_img, stride=8), :] for i in range(g_proj.shape[-1] * 2 // 128)]
    pooled = jnp.concatenate(pooled, 1).astype(bf16)
    proj_all = g_proj[...].reshape(n_img * 8, g_proj.shape[-1])
    cut = g_proj.shape[-1]
    n_emb = proj_all.shape[0]
    low = dot(pooled[:, :cut], proj_all, 1, 1)
    high = dot(pooled[:, cut:], proj_all, 1, 1)
    real = iota(low.shape, 1) % 8 < cols_dev
    projected = jnp.where(real, low + pltpu.roll(high, n_emb - cols_dev, 1), 0.0)
    proj_norm = jnp.sqrt(jnp.sum(projected * projected, -1, keepdims=True) + 1e-06)
    image_emb = projected / proj_norm
    parts = [captions[:, :, z].reshape(n_img, 128) for z in range(4)]
    squares = sum(jnp.sum(part * part, -1, keepdims=True) for part in parts)
    size = 128 // cols_dev * 8
    row, col = iota((128, size), 0), iota((128, size), 1)
    chosen = jnp.where((row == col // 8 * cols_dev + col % 8) & (col % 8 < cols_dev), 1.0, 0.0)
    caption_all = jnp.concatenate([exact(part, chosen, 1, 0) for part in parts], 1)
    caption_all = caption_all / jnp.sqrt(squares + 1e-06)
    scores = 100.0 * exact(image_emb, caption_all, 1, 1)
    match = jnp.where(iota(scores.shape, 1) == target_of[...], 1.0, 0.0)

    def soft(axis):
        top = jnp.max(scores, axis, keepdims=True)
        powers = jnp.exp(scores - top)
        total = jnp.sum(powers, axis, keepdims=True)
        return jnp.sum(top + jnp.log(total)), powers / total

    log_rows, soft_rows = soft(1)
    log_cols, soft_cols = soft(0)
    contrast = log_rows + log_cols - 2.0 * jnp.sum(match * scores)
    grad_scores = soft_rows + soft_cols - 2.0 * match
    grad_image = 100.0 * exact(grad_scores, caption_all, 1, 0)
    inner = jnp.sum(image_emb * grad_image, -1, keepdims=True)
    grad_projected = ((grad_image - image_emb * inner) / proj_norm).astype(bf16)
    grad_img[...] = grad_projected.astype(f32)
    row, col = iota((n_emb, 128), 0), iota((n_emb, 128), 1)
    chosen = jnp.where((row == 8 * shard + col) & (col < cols_dev), 1.0, 0.0).astype(bf16)
    columns = dot(grad_projected, chosen, 1, 0).astype(bf16)
    o_proj[...] = dot(columns, pooled, 0, 0)[:cols_dev]
    mine = jnp.broadcast_to(grad_img[pl.ds(shard, 1), :], (8, n_emb))
    grad_low = dot(mine.astype(bf16), proj_all, 1, 0)
    grad_high = dot(pltpu.roll(mine, cols_dev, 1).astype(bf16), proj_all, 1, 0)
    grad_pooled = jnp.concatenate([grad_low, grad_high], 1)[:1]

    s_acc[...] = jnp.zeros_like(s_acc)
    f_tile[...] = jnp.zeros_like(f_tile)

    def head_block(n, carry):
        weights = g_head[n // 4, n % 4].reshape(step, -1)
        cols = pl.ds(pl.multiple_of(n * step, step), step)
        lanes = pl.ds(pl.multiple_of(n % 2 * step, step), step)
        pred = dot(rounded[...], weights, 1, 1)
        added = near[n // 2, :, lanes].astype(f32) + got[n // 2, :, lanes].astype(f32)
        diff = pred - (wide[:, cols].astype(f32) + added)
        f_tile[...] = f_tile[...] + jnp.sum(diff * diff)
        grad_pred = (2.0 * diff / width).astype(bf16)
        d_head[n // 4, n % 4] = (
            dot(grad_pred, rounded[...], 0, 0).astype(bf16).reshape(d_head.shape[2:])
        )
        s_acc[...] = s_acc[...] + dot(grad_pred, weights, 1, 0)
        return carry

    for y in range(4):
        exchange[y].wait_recv()
        lax.fori_loop(2 * y, 2 * y + 2, head_block, 0)

    scatter = Scatter(copies, me, sibling, d_pack, d_head, accs, hold)
    scatter.push(1)
    grad_out[...] = (s_acc[...] + grad_pooled / PATCHES).astype(bf16)

    def pack_block(n, carry):
        weights = g_pack[n // 4, n % 4].reshape(-1, g_pack.shape[-1])
        size = weights.shape[0]
        cols = pl.ds(pl.multiple_of(n * size, 128), size)
        grad_act = pltpu.roll(dot(grad_out[...], weights, 1, 1), size - hid, 1)
        grad_gate = jax.vjp(gelu_tanh, gates[:, cols])[1](grad_act)[0]
        grad_gate = jnp.where(ups(grad_gate.shape), grad_gate, 0.0).astype(bf16)
        total = dot(grad_gate, normed[...], 0, 0) + dot(acts[:, cols], grad_out[...], 0, 0)
        d_pack[n // 4, n % 4] = total.astype(bf16).reshape(d_pack.shape[2:])
        return carry

    lax.fori_loop(0, 8, pack_block, 0)
    scatter.push(0)
    f_tile[...] = f_tile[...] / width
    total = scatter.finish(f_tile, s_slots, o_up, o_down, o_head)
    o_loss[...] = (total + contrast) / (n_img * PATCHES)
    copies.finish()


N_COPIES = 22 * 3 + 19 + 4 * 15 + 4 * 16 + 10 + 4 + 70


def run_step(t_up, t_down, up, down, head, proj, words, t_in, t_gain, s_in, s_gain, target_of):
    bf16, f32 = t_up.dtype, jnp.float32
    rows, width = t_in.shape[0], up.shape[1]
    own_rows = rows // 2
    hid, feat = up.shape[0], head.shape[0]
    whole = (2, 4, 2, 4, 2)
    tiles = (4, 4, 4, 8, 128)
    teacher = (4, 2, 4, 2, 2 * BLK, t_up.shape[1])
    n_wide = 128 * BLK
    n_pack = 128 * 2 * hid
    vmem = pltpu.VMEM
    scratch = [
        vmem(teacher, bf16),
        vmem(teacher, bf16),
        vmem(whole + (2 * hid, width), bf16),
        vmem(whole + (BLK, width), bf16),
        vmem(whole + (2 * proj.shape[0], width // 2), bf16),
        vmem(tiles, f32),
        vmem(whole + (8, 128), f32),
        vmem((own_rows, n_pack), f32),
        vmem((own_rows, n_pack), bf16),
        vmem((own_rows, width), bf16),
        vmem((own_rows, width), bf16),
        vmem((own_rows, n_wide), bf16),
        vmem((4, own_rows, n_wide // 4), bf16),
        vmem((4, own_rows, n_wide // 4), bf16),
        vmem((4, own_rows, n_wide // 4), bf16),
        vmem((rows, n_wide), bf16),
        vmem((rows, t_up.shape[1]), bf16),
        vmem((own_rows, width), f32),
        vmem((own_rows, width), bf16),
        vmem((128, 128 * 8), f32),
        vmem(whole + (2 * hid, width), bf16),
        vmem(whole + (BLK, width), bf16),
        vmem((8, 128), f32),
        vmem(tiles, f32),
        vmem((5, 4, 4, 8, 128), f32),
        vmem((5, 4, 8, 128), f32),
        vmem((4, 8, 128), f32),
        vmem((4, 4, 8, 128), f32),
        pltpu.SemaphoreType.DMA((N_COPIES,)),
        pltpu.SemaphoreType.DMA((N_COPIES,)),
    ]
    block = 2 * hid + BLK
    scratch += [vmem((2, 4, 2, 4, block, COLS), bf16) for _ in range(3)]
    for t in range(3):
        for phase in range(3):
            scratch.append(vmem((2,) + half_shape(ORDERS[t], phase, block), bf16))
            scratch.append(vmem((2,) + dims_of(rest_of(ORDERS[t], phase)) + (block, COLS), bf16))
    return pl.pallas_call(
        step_kernel,
        out_shape=[
            jax.ShapeDtypeStruct(s, f32)
            for s in ((hid, width), (hid, width), (feat, width), (proj.shape[0], width), (8, 128))
        ],
        in_specs=[VM] * 12,
        out_specs=[VM] * 5,
        scratch_shapes=scratch,
        compiler_params=pltpu.CompilerParams(
            collective_id=1, has_side_effects=True, vmem_limit_bytes=67043328
        ),
        name="step",
    )(
        t_up, t_down, up, down, head, proj,
        words.reshape(16, 8, 4, 128).transpose(0, 2, 1, 3).reshape(tiles),
        t_in, t_gain.reshape(1, -1), s_in, s_gain.reshape(1, -1), target_of,
    )


def local(
    teacher_in,
    teacher_gain,
    teacher_up,
    teacher_down,
    student_in,
    student_gain,
    student_up,
    student_down,
    student_head,
    student_proj,
    word_table,
    caption_ids,
    positive,
):
    grp_index = lax.axis_index("grp")
    dp_index = lax.axis_index("dp")
    n_grp = lax.axis_size("grp")
    n_dp = lax.axis_size("dp")
    shard = grp_index * n_dp + dp_index
    vocab_dev = word_table.shape[0]
    vocab_codes = shard * vocab_dev + jnp.arange(vocab_dev, dtype=jnp.int32)
    counts = jnp.sum(
        caption_ids[:, :, None] == vocab_codes[None, None, :], 1, dtype=jnp.float32
    ).astype(jnp.bfloat16)
    partial_words = jnp.dot(counts, word_table, preferred_element_type=jnp.float32) / CAP_LEN

    target_of = positive.reshape(n_dp, n_grp).T.reshape(-1, 1)
    grad_up, grad_down, grad_head, grad_proj, loss = run_step(
        teacher_up,
        teacher_down,
        student_up.T,
        student_down,
        student_head.T,
        student_proj.T,
        partial_words,
        teacher_in,
        teacher_gain,
        student_in,
        student_gain,
        target_of,
    )
    return (loss[0, 0], grad_up.T, grad_down, grad_head.T, grad_proj.T)


def solution(mesh):
    placed = (
        P("dp", None),
        P(),
        P("dp", "grp"),
        P("dp", "grp"),
        P("dp", None),
        P(),
        P(None, ("grp", "dp")),
        P(("grp", "dp"), None),
        P(None, ("grp", "dp")),
        P(None, ("grp", "dp")),
        P(("grp", "dp"), None),
        P(),
        P(),
    )
    return jax.shard_map(
        local,
        mesh=mesh,
        in_specs=placed,
        out_specs=(
            P(),
            P(None, ("grp", "dp")),
            P(("grp", "dp"), None),
            P(None, ("grp", "dp")),
            P(None, ("grp", "dp")),
        ),
        check_vma=False,
    )
```

profile of v0, /device:TPU:0, one launch (start us, length us, event | category | flops | bytes accessed | tf_op | source)
XLA Modules:
  0.0 172.0 jit_solution(7742381237749360166)
XLA Ops:
  0.6 1.3 reshape.36.s_gain
  1.9 1.3 reshape.35.t_gain
  3.2 0.8 reshape.37
  4.0 0.1 copy.24
  4.1 0.8 reshape.39.target_of
  4.8 2.4 %convert_reduce_fusion = bf16[128,386]{0,1:T(8,128)(2,1)S(1)} fusion(s32[128,77]{0,1:T(8,128)} %param.24, s32[386]{0:T(512)S(1)} %iota_add_fusion), kind=kLoop, calls=%fused_computation | loop fusion | flops 15168256 | bytes 139784 | tf_op jit(solution)/shard_map/reduce_sum | solution.py:751
  7.3 1.9 %convolution_multiply_fusion = f32[128,512]{1,0:T(8,128)} fusion(bf16[386,512]{1,0:T(8,128)(2,1)} %param.23, bf16[128,386]{0,1:T(8,128)(2,1)S(1)} %convert_reduce_fusion), kind=kOutput, calls=%fused_computation.1 | convolution fusion | flops 50659328 | bytes 756224 | tf_op jit(solution)/shard_map/dot_general | solution.py:754
  9.2 156.0 %step.1 = (f32[12,768]{1,0:T(8,128)}, f32[12,768]{1,0:T(8,128)}, f32[13,768]{1,0:T(8,128)}, f32[4,768]{1,0:T(4,128)}, f32[8,128]{1,0:T(8,128)}) custom-call(bf16[26,2048]{1,0:T(8,128)(2,1)} %t_up.1, bf16[26,2048]{1,0:T(8,128)(2,1)} %t_down.1, bf16[12,768]{1,0:T(8,128)(2,1)} %bitcast.19, bf16[12,768]{1,0:T(8,128)(2,1)} %down.1, bf16[13,768]{1,0:T(8,128)(2,1)} %bitcast.20, ...), custom_call_target="tpu_custom_call" | custom-call | tf_op jit(solution)/shard_map/step/pallas_call | solution.py:709
  165.3 1.2 slice.3
  166.5 1.4 copy.30
  167.9 1.4 copy.31
  169.3 1.4 copy.32
  170.7 1.3 copy.33
  (1 shorter events, 0.0 us)
where the time goes:
time: 173 us; the launch traced here: 172 us
  Pallas kernels  156 us (90%)
  local copies, waits for them, and re-layouts  11 us (6%)
  other arithmetic  2.43 us (1%)
  matrix products  1.94 us (1%)
    pallas_call x1, Pallas kernels, run_step(): pl.pallas_call(step_kernel, out_shape=[jax.ShapeDtypeStruct(s, f32) for s...  156 us
    unnamed x4, local copies, waits for them, and re-layouts  5.57 us

commit v1 on v0

--- a/solution.py
+++ b/solution.py
@@ -286,51 +286,49 @@
 
 
 class Scatter:
-    def __init__(self, copies, me, sibling, pack, head, accs, hold):
+    def __init__(self, copies, me, sibling, ref, accs, hold):
         self.copies, self.me, self.sibling = copies, me, sibling
-        self.pack, self.head, self.accs, self.hold = pack, head, accs, hold
+        self.ref, self.accs, self.hold = ref, accs, hold
         self.opening = {}
+        self.sums = [None] * 3
 
     def first(self, t, phase):
-        return self.hold[(t * 3 + phase) * 2]
+        return self.hold[t * 5 + phase * 2]
 
     def second(self, t, phase):
-        return self.hold[(t * 3 + phase) * 2 + 1]
-
-    def source(self, which, t, at):
-        ref = self.head if which else self.pack
-        return rows_of(pick(ref, at), 0, ref.shape[-2], pl.ds(t * COLS, COLS))
-
-    def place(self, which, t, at):
-        n_pack = self.pack.shape[-2]
-        first, count = (n_pack, self.head.shape[-2]) if which else (0, n_pack)
-        return rows_of(pick(self.accs[t], at), first, count)
+        return self.hold[t * 5 + (phase * 2 + 1 if phase < 2 else 4)]
+
+    def source(self, t, at):
+        return rows_of(pick(self.ref, at), 0, self.ref.shape[-2], pl.ds(t * COLS, COLS))
 
     def at(self, t, step):
         axis = ORDERS[t][0]
         return {axis: shifted(self.me, axis, step)[axis]}
 
-    def push(self, which):
+    def push(self):
         for step in (2, 1, 3, 0):
             for t in range(3):
                 at = self.at(t, step)
-                self.opening[which, t, step] = self.copies.start(
-                    self.source(which, t, {**at, "core": self.sibling["core"]}),
-                    self.place(which, t, at),
+                self.opening[t, step] = self.copies.start(
+                    self.source(t, {**at, "core": self.sibling["core"]}),
+                    pick(self.accs[t], at),
                     self.sibling,
                 )
 
     def opened(self, t, step):
         at = self.at(t, step)
-        for which in range(2):
-            self.opening[which, t, step].wait_recv()
-            add_into(
-                self.place(which, t, at),
-                [self.source(which, t, {**at, "core": self.me["core"]})],
-            )
+        self.opening[t, step].wait_recv()
+        add_into(pick(self.accs[t], at), [self.source(t, {**at, "core": self.me["core"]})])
 
     def open_phase(self, t, phase, held):
         axis = ORDERS[t][phase]
+        if phase == 2:
+            waits = []
+            for step in (2, 1, 3):
+                peer = shifted(self.me, axis, step)
+                view = pick(self.accs[t], {**held, axis: peer[axis]})
+                waits.append(self.copies.start(view, self.second(t, 2).at[step - 1], peer))
+            return waits
         far = shifted(self.me, axis, 2)
         view = pick(self.accs[t], {**held, axis: far[axis]})
         up, down = shifted(self.me, axis, 1), shifted(self.me, axis, 3)
@@ -339,11 +337,8 @@
             self.copies.start(half(view, 1), self.first(t, phase).at[1], down),
         )
 
-    def finish(self, s_ref, s_slots, o_up, o_down, o_head):
-        copies, me, accs = self.copies, self.me, self.accs
-        n_pack = self.pack.shape[-2]
-        s_wait = [copies.start(s_ref, s_slots.at[0, me["core"]], self.sibling)]
-        s_slots[0, me["core"]] = s_ref[...]
+    def chain(self):
+        me, accs = self.me, self.accs
         pending = [None] * 3
         held = [dict() for _ in range(3)]
         for t in range(3):
@@ -352,16 +347,8 @@
         for step in (1, 3, 0):
             for t in range(3):
                 self.opened(t, step)
-        for copy in s_wait:
-            copy.wait_recv()
-        s_value = s_slots[0, 0] + s_slots[0, 1]
-        for phase in range(3):
-            s_axis = ("x", "y", "z")[phase]
-            s_slots[phase + 1, me[s_axis]] = s_value
-            s_wait = []
-            for step in (1, 2, 3):
-                s_mine = s_slots.at[phase + 1, me[s_axis]]
-                s_wait.append(copies.start(s_mine, s_mine, shifted(me, s_axis, step)))
+        for phase in range(2):
+            yield
             for t in range(3):
                 axis = ORDERS[t][phase]
                 up, down = shifted(me, axis, 1), shifted(me, axis, 3)
@@ -369,35 +356,48 @@
                 to_down = pick(accs[t], {**held[t], axis: down[axis]})
                 pending[t][0].wait_recv()
                 add_into(half(to_up, 0), [self.first(t, phase).at[0]])
-                a = copies.start(to_up, self.second(t, phase).at[0], up)
+                a = self.copies.start(to_up, self.second(t, phase).at[0], up)
                 pending[t][1].wait_recv()
                 add_into(half(to_down, 1), [self.first(t, phase).at[1]])
-                b = copies.start(to_down, self.second(t, phase).at[1], down)
+                b = self.copies.start(to_down, self.second(t, phase).at[1], down)
                 pending[t] = (a, b)
+            yield
             for t in range(3):
                 axis = ORDERS[t][phase]
                 pending[t][0].wait_recv()
                 pending[t][1].wait_recv()
                 held[t][axis] = me[axis]
-                mine = pick(accs[t], held[t])
                 got = self.second(t, phase)
-                if phase < 2:
-                    add_into(mine, [got.at[0], got.at[1]])
-                    pending[t] = self.open_phase(t, phase + 1, held[t])
-                else:
-                    value = mine[...].astype(jnp.float32) + got[0].astype(jnp.float32)
-                    value = value + got[1].astype(jnp.float32)
-                    cols = pl.ds(t * COLS, COLS)
-                    hid = o_up.shape[0]
-                    o_up[:, cols] = value[:hid]
-                    o_down[:, cols] = value[hid:n_pack]
-                    o_head[:, cols] = value[n_pack : n_pack + o_head.shape[0]]
-            for copy in s_wait:
+                add_into(pick(accs[t], held[t]), [got.at[0], got.at[1]])
+                pending[t] = self.open_phase(t, phase + 1, held[t])
+        yield
+        for t in range(3):
+            for copy in pending[t]:
                 copy.wait_recv()
-            s_value = (s_slots[phase + 1, 0] + s_slots[phase + 1, 1]) + (
-                s_slots[phase + 1, 2] + s_slots[phase + 1, 3]
-            )
-        return s_value
+            axis = ORDERS[t][2]
+            value = pick(accs[t], {**held[t], axis: me[axis]})[...].astype(jnp.float32)
+            for slot in range(3):
+                value = value + self.second(t, 2)[slot].astype(jnp.float32)
+            self.sums[t] = value
+
+
+def scalar_chain(copies, me, sibling, tile, slots):
+    waits = [copies.start(tile, slots.at[0, me["core"]], sibling)]
+    slots[0, me["core"]] = tile[...]
+    value = None
+    for phase, axis in enumerate(("x", "y", "z", None)):
+        yield
+        for copy in waits:
+            copy.wait_recv()
+        value = slots[phase, 0] + slots[phase, 1]
+        if phase:
+            value = value + (slots[phase, 2] + slots[phase, 3])
+        if axis is None:
+            break
+        mine = slots.at[phase + 1, me[axis]]
+        mine[...] = value
+        waits = [copies.start(mine, mine, shifted(me, axis, step)) for step in (2, 1, 3)]
+    slots[4, 0] = value
 
 
 def gelu_tanh(values):
@@ -416,19 +416,18 @@
 
 
 ORDER = (
-    "PHQuKUvVDdnnPHKQnuUnPHQvdDnKuUeEVHQPveEuKUVPvEeuUVDdeKuUvEV",
-    "PHQdDePKEvVPssdssvsVssKDsSIehdhhIHDEehhhhhE",
+    "PuUVCKvDdHQnnnPnUuDnVdHPQKvUuEeVHvPQEeUuKVHvDdQPeEUuUKuVv",
+    "HdEPDQevVKdHvVhEdhhehhKDhhhPDEQePssEssessHsQsSKHQ",
 )
 
 
 def step_kernel(
-    t_up, t_down, up, down, head, proj, words, t_in, t_gain, s_in, s_gain, target_of,
+    t_up, t_down, up, down, head, proj, table, ids, t_in, t_gain, s_in, s_gain, positive,
     o_up, o_down, o_head, o_proj, o_loss,
     g_up, g_down, g_pack, g_head, g_proj, captions, images, gates, acts, normed, rounded, wide,
     far, near, got, t_normed, t_act, s_acc, grad_out, grad_img, d_pack, d_head, f_tile,
-    other, at_x, at_y, at_z, s_slots, send, recv, *stores
+    words, other, at_x, at_y, at_z, s_slots, send, recv, *stores
 ):
-    accs, hold = stores[:3], stores[3:]
     me = coords()
     grp = me["x"] % 2
     shard = grp * 64 + me["y"] * 16 + me["x"] // 2 * 8 + me["z"] * 2 + me["core"]
@@ -478,13 +477,25 @@
     step = 256
     span = step // BLK * feat
 
+    def count_words():
+        vocab = table.shape[0]
+        code = iota((vocab, ids.shape[1]), 0) + shard * vocab
+
+        def body(j, counts):
+            return counts + jnp.where(code == ids[pl.ds(j, 1), :], 1.0, 0.0)
+
+        counts = lax.fori_loop(0, ids.shape[0], body, jnp.zeros(code.shape, f32))
+        sums = dot(counts.astype(bf16), table[...], 0, 0) / CAP_LEN
+        for z in range(4):
+            words[:, :, z] = sums[:, z * 128 : (z + 1) * 128].reshape(4, 4, 8, 128)
+
     def student_norm():
-        normed[...] = norm_rows(s_in[own, :].astype(f32), s_gain[...])
+        normed[...] = norm_rows(s_in[own, :].astype(f32), s_gain[...].reshape(1, -1))
 
     def teacher_norm():
         def body(r, carry):
             rows = pl.ds(pl.multiple_of(r * 64, 64), 64)
-            t_act[rows, pl.ds(0, width)] = norm_rows(t_in[rows, :].astype(f32), t_gain[...])
+            t_act[rows, pl.ds(0, width)] = norm_rows(t_in[rows, :].astype(f32), t_gain[...].reshape(1, -1))
             return carry
 
         lax.fori_loop(0, t_in.shape[0] // 64, body, 0)
@@ -534,6 +545,7 @@
         pick(images, me)[...] = tile.astype(bf16).astype(f32)
 
     work = {
+        "C": [count_words],
         "n": [student_norm, teacher_norm]
         + [lambda k=k: [spread(j) for j in range(k, k + 3) if j < 8] for k in (0, 3, 6)],
         "h": [lambda j=j: hidden(j) for j in range(8)],
@@ -549,18 +561,50 @@
 
     partner = {**me, "x": me["x"] + 1 - 2 * grp}
     exchange = []
+    next(chains["I"], None)
+    branch(0, partner_rows, far)
+    branch(1, partner_rows, far)
+    next(chains["I"], None)
     for y in range(4):
-        branch(y, partner_rows, far)
+        if y > 1:
+            branch(y, partner_rows, far)
         exchange.append(copies.start(far.at[y], got.at[y], partner))
-    next(chains["I"], None)
     branch(0, own, near)
     branch(1, own, near)
     next(chains["I"], None)
     branch(2, own, near)
     branch(3, own, near)
+    images_left = chains.pop("I")
     for turn in range(8):
         for one in chains.values():
             next(one, None)
+    next(images_left, None)
+
+    s_acc[...] = jnp.zeros_like(s_acc)
+    f_tile[...] = jnp.zeros_like(f_tile)
+
+    def head_block(n, carry):
+        weights = g_head[n // 4, n % 4].reshape(step, -1)
+        cols = pl.ds(pl.multiple_of(n * step, step), step)
+        lanes = pl.ds(pl.multiple_of(n % 2 * step, step), step)
+        pred = dot(rounded[...], weights, 1, 1)
+        added = near[n // 2, :, lanes].astype(f32) + got[n // 2, :, lanes].astype(f32)
+        diff = pred - (wide[:, cols].astype(f32) + added)
+        f_tile[...] = f_tile[...] + jnp.sum(diff * diff)
+        grad_pred = (2.0 * diff / width).astype(bf16)
+        d_head[n // 4, n % 4] = (
+            dot(grad_pred, rounded[...], 0, 0).astype(bf16).reshape(d_head.shape[2:])
+        )
+        s_acc[...] = s_acc[...] + dot(grad_pred, weights, 1, 0)
+        return carry
+
+    def head_blocks(y):
+        exchange[y].wait_recv()
+        lax.fori_loop(2 * y, 2 * y + 2, head_block, 0)
+
+    head_blocks(0)
+    head_blocks(1)
+    next(images_left, None)
 
     n_img = 128
     cols_dev = o_proj.shape[0]
@@ -584,7 +628,11 @@
     caption_all = jnp.concatenate([exact(part, chosen, 1, 0) for part in parts], 1)
     caption_all = caption_all / jnp.sqrt(squares + 1e-06)
     scores = 100.0 * exact(image_emb, caption_all, 1, 1)
-    match = jnp.where(iota(scores.shape, 1) == target_of[...], 1.0, 0.0)
+    target = jnp.broadcast_to(positive[...].reshape(1, -1), (n_img, n_img))
+    match = jnp.where(iota(target.shape, 0) == target, 1.0, 0.0).astype(bf16)
+    row = iota(target.shape, 0)
+    chosen = jnp.where(iota(target.shape, 1) == row % 64 * 2 + row // 64, 1.0, 0.0).astype(bf16)
+    match = dot(chosen, match, 1, 1)
 
     def soft(axis):
         top = jnp.max(scores, axis, keepdims=True)
@@ -609,30 +657,14 @@
     grad_high = dot(pltpu.roll(mine, cols_dev, 1).astype(bf16), proj_all, 1, 0)
     grad_pooled = jnp.concatenate([grad_low, grad_high], 1)[:1]
 
-    s_acc[...] = jnp.zeros_like(s_acc)
-    f_tile[...] = jnp.zeros_like(f_tile)
-
-    def head_block(n, carry):
-        weights = g_head[n // 4, n % 4].reshape(step, -1)
-        cols = pl.ds(pl.multiple_of(n * step, step), step)
-        lanes = pl.ds(pl.multiple_of(n % 2 * step, step), step)
-        pred = dot(rounded[...], weights, 1, 1)
-        added = near[n // 2, :, lanes].astype(f32) + got[n // 2, :, lanes].astype(f32)
-        diff = pred - (wide[:, cols].astype(f32) + added)
-        f_tile[...] = f_tile[...] + jnp.sum(diff * diff)
-        grad_pred = (2.0 * diff / width).astype(bf16)
-        d_head[n // 4, n % 4] = (
-            dot(grad_pred, rounded[...], 0, 0).astype(bf16).reshape(d_head.shape[2:])
-        )
-        s_acc[...] = s_acc[...] + dot(grad_pred, weights, 1, 0)
-        return carry
-
-    for y in range(4):
-        exchange[y].wait_recv()
-        lax.fori_loop(2 * y, 2 * y + 2, head_block, 0)
-
-    scatter = Scatter(copies, me, sibling, d_pack, d_head, accs, hold)
-    scatter.push(1)
+    head_blocks(2)
+    head_blocks(3)
+    n_store = len(stores) // 2
+    head_sums = Scatter(copies, me, sibling, d_head, stores[:3], stores[3:n_store])
+    pack_sums = Scatter(copies, me, sibling, d_pack, stores[n_store : n_store + 3], stores[n_store + 3 :])
+    head_sums.push()
+    f_tile[...] = f_tile[...] / width
+    ends = [head_sums.chain(), scalar_chain(copies, me, sibling, f_tile, s_slots)]
     grad_out[...] = (s_acc[...] + grad_pooled / PATCHES).astype(bf16)
 
     def pack_block(n, carry):
@@ -646,18 +678,28 @@
         d_pack[n // 4, n % 4] = total.astype(bf16).reshape(d_pack.shape[2:])
         return carry
 
-    lax.fori_loop(0, 8, pack_block, 0)
-    scatter.push(0)
-    f_tile[...] = f_tile[...] / width
-    total = scatter.finish(f_tile, s_slots, o_up, o_down, o_head)
-    o_loss[...] = (total + contrast) / (n_img * PATCHES)
+    for part in range(4):
+        lax.fori_loop(2 * part, 2 * part + 2, pack_block, 0)
+        for one in ends:
+            next(one, None)
+    pack_sums.push()
+    ends.append(pack_sums.chain())
+    for turn in range(8):
+        for one in ends:
+            next(one, None)
+    for t in range(3):
+        cols = pl.ds(t * COLS, COLS)
+        o_up[:, cols] = pack_sums.sums[t][:hid]
+        o_down[:, cols] = pack_sums.sums[t][hid:]
+        o_head[:, cols] = head_sums.sums[t][:feat]
+    o_loss[...] = (s_slots[4, 0] + contrast) / (n_img * PATCHES)
     copies.finish()
 
 
-N_COPIES = 22 * 3 + 19 + 4 * 15 + 4 * 16 + 10 + 4 + 70
-
-
-def run_step(t_up, t_down, up, down, head, proj, words, t_in, t_gain, s_in, s_gain, target_of):
+N_COPIES = 22 * 3 + 19 + 4 * 15 + 4 * 16 + 10 + 4 + 10 + 2 * 45
+
+
+def run_step(t_up, t_down, up, down, head, proj, table, ids, t_in, t_gain, s_in, s_gain, positive):
     bf16, f32 = t_up.dtype, jnp.float32
     rows, width = t_in.shape[0], up.shape[1]
     own_rows = rows // 2
@@ -693,37 +735,48 @@
         vmem(whole + (BLK, width), bf16),
         vmem((8, 128), f32),
         vmem(tiles, f32),
+        vmem(tiles, f32),
         vmem((5, 4, 4, 8, 128), f32),
         vmem((5, 4, 8, 128), f32),
         vmem((4, 8, 128), f32),
-        vmem((4, 4, 8, 128), f32),
+        vmem((5, 4, 8, 128), f32),
         pltpu.SemaphoreType.DMA((N_COPIES,)),
         pltpu.SemaphoreType.DMA((N_COPIES,)),
     ]
-    block = 2 * hid + BLK
-    scratch += [vmem((2, 4, 2, 4, block, COLS), bf16) for _ in range(3)]
-    for t in range(3):
-        for phase in range(3):
-            scratch.append(vmem((2,) + half_shape(ORDERS[t], phase, block), bf16))
-            scratch.append(vmem((2,) + dims_of(rest_of(ORDERS[t], phase)) + (block, COLS), bf16))
-    return pl.pallas_call(
+    for block in (BLK, 2 * hid):
+        scratch += [vmem((2, 4, 2, 4, block, COLS), bf16) for _ in range(3)]
+        for order in ORDERS:
+            for phase in range(2):
+                rest = dims_of(rest_of(order, phase)) + (block, COLS)
+                scratch.append(vmem((2,) + half_shape(order, phase, block), bf16))
+                scratch.append(vmem((2,) + rest, bf16))
+            scratch.append(vmem((3, block, COLS), bf16))
+    shapes = [(hid, width), (hid, width), (feat, width), (proj.shape[0], width), (8, 128)]
+    shapes = [jax.ShapeDtypeStruct(shape, f32) for shape in shapes]
+    out = pl.pallas_call(
         step_kernel,
-        out_shape=[
-            jax.ShapeDtypeStruct(s, f32)
-            for s in ((hid, width), (hid, width), (feat, width), (proj.shape[0], width), (8, 128))
-        ],
-        in_specs=[VM] * 12,
+        out_shape=shapes,
+        in_specs=[VM] * 13,
         out_specs=[VM] * 5,
         scratch_shapes=scratch,
         compiler_params=pltpu.CompilerParams(
             collective_id=1, has_side_effects=True, vmem_limit_bytes=67043328
         ),
         name="step",
-    )(
-        t_up, t_down, up, down, head, proj,
-        words.reshape(16, 8, 4, 128).transpose(0, 2, 1, 3).reshape(tiles),
-        t_in, t_gain.reshape(1, -1), s_in, s_gain.reshape(1, -1), target_of,
-    )
+    )(t_up, t_down, up, down, head, proj, table, ids, t_in, t_gain, s_in, s_gain, positive)
+    return pl.pallas_call(
+        write_kernel,
+        out_shape=shapes[:4] + [jax.ShapeDtypeStruct((1, 1), f32)],
+        in_specs=[VM] * 5,
+        out_specs=[VM] * 4 + [pl.BlockSpec(memory_space=pltpu.SMEM)],
+        name="write",
+    )(*out)
+
+
+def write_kernel(*refs):
+    for source, out in zip(refs[:4], refs[5:9]):
+        out[...] = source[...]
+    refs[9][0, 0] = jnp.max(refs[4][...])
 
 
 def local(
@@ -741,19 +794,6 @@
     caption_ids,
     positive,
 ):
-    grp_index = lax.axis_index("grp")
-    dp_index = lax.axis_index("dp")
-    n_grp = lax.axis_size("grp")
-    n_dp = lax.axis_size("dp")
-    shard = grp_index * n_dp + dp_index
-    vocab_dev = word_table.shape[0]
-    vocab_codes = shard * vocab_dev + jnp.arange(vocab_dev, dtype=jnp.int32)
-    counts = jnp.sum(
-        caption_ids[:, :, None] == vocab_codes[None, None, :], 1, dtype=jnp.float32
-    ).astype(jnp.bfloat16)
-    partial_words = jnp.dot(counts, word_table, preferred_element_type=jnp.float32) / CAP_LEN
-
-    target_of = positive.reshape(n_dp, n_grp).T.reshape(-1, 1)
     grad_up, grad_down, grad_head, grad_proj, loss = run_step(
         teacher_up,
         teacher_down,
@@ -761,12 +801,13 @@
         student_down,
         student_head.T,
         student_proj.T,
-        partial_words,
+        word_table,
+        caption_ids.T,
         teacher_in,
         teacher_gain,
         student_in,
         student_gain,
-        target_of,
+        positive,
     )
     return (loss[0, 0], grad_up.T, grad_down, grad_head.T, grad_proj.T)
 

time: 173 us -> 153 us (0.88)
  local copies, waits for them, and re-layouts: 11 us -> 0 us
  Pallas kernels: 156 us -> 152 us
  other arithmetic: 2.43 us -> 0 us
  matrix products: 1.94 us -> 0 us
    unnamed x4 -> x0, local copies, waits for them, and re-layouts: 5.57 us -> none
    reshape x4 -> x0, local copies, waits for them, and re-layouts: 4.12 us -> none  [the longest x2 1.56 us: local(): target_of = positive.reshape(n_dp, n_grp).T.reshape(-1, 1)]
    pallas_call x1 -> x2, Pallas kernels: 156 us -> 152 us  [the longest x1 151 us: run_step(): pl.pallas_call(step_kernel, out_shape=shapes, in_specs=[VM] * 13, out_spe...]
    reduce_sum x1 -> x0, other arithmetic: 2.43 us -> none  [local(): jnp.sum(caption_ids[:, :, None] == vocab_codes[None, None, :], 1, dtype=j...]
    dot_general x1 -> x0, matrix products: 1.94 us -> none  [local(): jnp.dot(counts, word_table, preferred_element_type=jnp.float32) / CAP_LEN]
where the time goes in v1:
time: 153 us
  Pallas kernels  152 us (99%)
    pallas_call x1, Pallas kernels, run_step(): pl.pallas_call(step_kernel, out_shape=shapes, in_specs=[VM] * 13, out_spe...  151 us

profile of v1, /device:TPU:0, one launch (start us, length us, event | category | flops | bytes accessed | tf_op | source)
XLA Modules:
  0.0 153.2 jit_solution(1518467054043553111)
XLA Ops:
  0.6 150.8 %step.1 = (f32[12,768]{1,0:T(8,128)}, f32[12,768]{1,0:T(8,128)}, f32[13,768]{1,0:T(8,128)}, f32[4,768]{1,0:T(4,128)}, f32[8,128]{1,0:T(8,128)}) custom-call(bf16[26,2048]{1,0:T(8,128)(2,1)} %t_up.1, bf16[26,2048]{1,0:T(8,128)(2,1)} %t_down.1, bf16[12,768]{1,0:T(8,128)(2,1)} %bitcast.9, bf16[12,768]{1,0:T(8,128)(2,1)} %down.1, bf16[13,768]{1,0:T(8,128)(2,1)} %bitcast.10, ...), custom_call_target="tpu_custom_call" | custom-call | tf_op jit(solution)/shard_map/step/pallas_call | solution.py:756
  151.5 1.5 %write.1 = (f32[12,768]{1,0:T(8,128)}, f32[12,768]{1,0:T(8,128)}, f32[13,768]{1,0:T(8,128)}, f32[4,768]{1,0:T(4,128)}, f32[1,1]{1,0:T(1,128)}) custom-call(f32[12,768]{1,0:T(8,128)} %get-tuple-element.15.refs_0_, f32[12,768]{1,0:T(8,128)} %get-tuple-element.16.refs_1_, f32[13,768]{1,0:T(8,128)} %get-tuple-element.17.refs_2_, ...), custom_call_target="tpu_custom_call" | custom-call | tf_op jit(solution)/shard_map/write/pallas_call | solution.py:767

commit v2 on v1

--- a/solution.py
+++ b/solution.py
@@ -42,7 +42,7 @@
             peers.append(shifted(me, axis, step))
     for peer in peers:
         pl.semaphore_signal(barrier, inc=1, device_id=device(peer), device_id_type=MESH)
-    pl.semaphore_wait(barrier, len(peers))
+    return lambda: pl.semaphore_wait(barrier, len(peers))
 
 
 class Copies:
@@ -253,7 +253,7 @@
 
 
 def add_into(dst, srcs):
-    lead = dst.shape[:-2]
+    lead = dst.shape[:-3]
     total = 1
     for size in lead:
         total *= size
@@ -265,7 +265,7 @@
         dst[index] = value.astype(dst.dtype)
 
     if total == 1:
-        one((0,) * len(lead) + (slice(None), slice(None)))
+        one((0,) * len(lead) + (Ellipsis,))
         return
 
     def body(n, carry):
@@ -292,11 +292,11 @@
         self.opening = {}
         self.sums = [None] * 3
 
-    def first(self, t, phase):
-        return self.hold[t * 5 + phase * 2]
+    def first(self, t):
+        return self.hold[t * 4]
 
     def second(self, t, phase):
-        return self.hold[t * 5 + (phase * 2 + 1 if phase < 2 else 4)]
+        return self.hold[t * 4 + 1 + phase]
 
     def source(self, t, at):
         return rows_of(pick(self.ref, at), 0, self.ref.shape[-2], pl.ds(t * COLS, COLS))
@@ -322,19 +322,19 @@
 
     def open_phase(self, t, phase, held):
         axis = ORDERS[t][phase]
-        if phase == 2:
+        if phase > 0:
             waits = []
             for step in (2, 1, 3):
                 peer = shifted(self.me, axis, step)
                 view = pick(self.accs[t], {**held, axis: peer[axis]})
-                waits.append(self.copies.start(view, self.second(t, 2).at[step - 1], peer))
+                waits.append(self.copies.start(view, self.second(t, phase).at[step - 1], peer))
             return waits
         far = shifted(self.me, axis, 2)
         view = pick(self.accs[t], {**held, axis: far[axis]})
         up, down = shifted(self.me, axis, 1), shifted(self.me, axis, 3)
         return (
-            self.copies.start(half(view, 0), self.first(t, phase).at[0], up),
-            self.copies.start(half(view, 1), self.first(t, phase).at[1], down),
+            self.copies.start(half(view, 0), self.first(t).at[0], up),
+            self.copies.start(half(view, 1), self.first(t).at[1], down),
         )
 
     def chain(self):
@@ -347,28 +347,28 @@
         for step in (1, 3, 0):
             for t in range(3):
                 self.opened(t, step)
+        yield
+        for t in range(3):
+            axis = ORDERS[t][0]
+            up, down = shifted(me, axis, 1), shifted(me, axis, 3)
+            to_up = pick(accs[t], {axis: up[axis]})
+            to_down = pick(accs[t], {axis: down[axis]})
+            pending[t][0].wait_recv()
+            add_into(half(to_up, 0), [self.first(t).at[0]])
+            a = self.copies.start(to_up, self.second(t, 0).at[0], up)
+            pending[t][1].wait_recv()
+            add_into(half(to_down, 1), [self.first(t).at[1]])
+            b = self.copies.start(to_down, self.second(t, 0).at[1], down)
+            pending[t] = (a, b)
         for phase in range(2):
             yield
             for t in range(3):
                 axis = ORDERS[t][phase]
-                up, down = shifted(me, axis, 1), shifted(me, axis, 3)
-                to_up = pick(accs[t], {**held[t], axis: up[axis]})
-                to_down = pick(accs[t], {**held[t], axis: down[axis]})
-                pending[t][0].wait_recv()
-                add_into(half(to_up, 0), [self.first(t, phase).at[0]])
-                a = self.copies.start(to_up, self.second(t, phase).at[0], up)
-                pending[t][1].wait_recv()
-                add_into(half(to_down, 1), [self.first(t, phase).at[1]])
-                b = self.copies.start(to_down, self.second(t, phase).at[1], down)
-                pending[t] = (a, b)
-            yield
-            for t in range(3):
-                axis = ORDERS[t][phase]
-                pending[t][0].wait_recv()
-                pending[t][1].wait_recv()
+                for copy in pending[t]:
+                    copy.wait_recv()
                 held[t][axis] = me[axis]
                 got = self.second(t, phase)
-                add_into(pick(accs[t], held[t]), [got.at[0], got.at[1]])
+                add_into(pick(accs[t], held[t]), [got.at[i] for i in range(len(pending[t]))])
                 pending[t] = self.open_phase(t, phase + 1, held[t])
         yield
         for t in range(3):
@@ -416,8 +416,8 @@
 
 
 ORDER = (
-    "PuUVCKvDdHQnnnPnUuDnVdHPQKvUuEeVHvPQEeUuKVHvDdQPeEUuUKuVv",
-    "HdEPDQevVKdHvVhEdhhehhKDhhhPDEQePssEssessHsQsSKHQ",
+    "VHvPDQdEeCKnnnHPuUKnDQVdnHPvuUQVEKHePvUuQVEePvuUKVvEDedu",
+    "UPQHuVvKUVEevhhhPhhhQhKhdDPssssEessssKESIedDIHQdDQ",
 )
 
 
@@ -437,6 +437,7 @@
     f32, bf16 = jnp.float32, jnp.bfloat16
     iota = lambda shape, axis: lax.broadcasted_iota(jnp.int32, shape, axis)
 
+    entered = enter(me)
     pick(g_pack, me)[...] = jnp.concatenate([up[...].astype(f32), down[...].astype(f32)], 0).astype(
         bf16
     )
@@ -451,7 +452,7 @@
             pick_teacher(out, me, (pl.ds(part * BLK, BLK),))[...] = rows_padded(cut, BLK).astype(
                 bf16
             )
-    enter(me)
+    entered()
     copies = Copies(send, recv)
 
     def teacher(ref, part, other_x):
@@ -561,24 +562,19 @@
 
     partner = {**me, "x": me["x"] + 1 - 2 * grp}
     exchange = []
+    for y in range(4):
+        branch(y, partner_rows, far)
+        exchange.append(copies.start(far.at[y], got.at[y], partner))
     next(chains["I"], None)
-    branch(0, partner_rows, far)
-    branch(1, partner_rows, far)
-    next(chains["I"], None)
-    for y in range(4):
-        if y > 1:
-            branch(y, partner_rows, far)
-        exchange.append(copies.start(far.at[y], got.at[y], partner))
     branch(0, own, near)
     branch(1, own, near)
+    branch(2, own, near)
     next(chains["I"], None)
-    branch(2, own, near)
     branch(3, own, near)
     images_left = chains.pop("I")
     for turn in range(8):
         for one in chains.values():
             next(one, None)
-    next(images_left, None)
 
     s_acc[...] = jnp.zeros_like(s_acc)
     f_tile[...] = jnp.zeros_like(f_tile)
@@ -603,7 +599,6 @@
         lax.fori_loop(2 * y, 2 * y + 2, head_block, 0)
 
     head_blocks(0)
-    head_blocks(1)
     next(images_left, None)
 
     n_img = 128
@@ -657,8 +652,8 @@
     grad_high = dot(pltpu.roll(mine, cols_dev, 1).astype(bf16), proj_all, 1, 0)
     grad_pooled = jnp.concatenate([grad_low, grad_high], 1)[:1]
 
-    head_blocks(2)
-    head_blocks(3)
+    for y in range(1, 4):
+        head_blocks(y)
     n_store = len(stores) // 2
     head_sums = Scatter(copies, me, sibling, d_head, stores[:3], stores[3:n_store])
     pack_sums = Scatter(copies, me, sibling, d_pack, stores[n_store : n_store + 3], stores[n_store + 3 :])
@@ -696,7 +691,7 @@
     copies.finish()
 
 
-N_COPIES = 22 * 3 + 19 + 4 * 15 + 4 * 16 + 10 + 4 + 10 + 2 * 45
+N_COPIES = 22 * 3 + 19 + 4 * 15 + 4 * 16 + 10 + 4 + 10 + 2 * 42
 
 
 def run_step(t_up, t_down, up, down, head, proj, table, ids, t_in, t_gain, s_in, s_gain, positive):
@@ -746,11 +741,10 @@
     for block in (BLK, 2 * hid):
         scratch += [vmem((2, 4, 2, 4, block, COLS), bf16) for _ in range(3)]
         for order in ORDERS:
-            for phase in range(2):
+            scratch.append(vmem((2,) + half_shape(order, 0, block), bf16))
+            for phase, count in enumerate((2, 3, 3)):
                 rest = dims_of(rest_of(order, phase)) + (block, COLS)
-                scratch.append(vmem((2,) + half_shape(order, phase, block), bf16))
-                scratch.append(vmem((2,) + rest, bf16))
-            scratch.append(vmem((3, block, COLS), bf16))
+                scratch.append(vmem((count,) + rest, bf16))
     shapes = [(hid, width), (hid, width), (feat, width), (proj.shape[0], width), (8, 128)]
     shapes = [jax.ShapeDtypeStruct(shape, f32) for shape in shapes]
     out = pl.pallas_call(

time: 153 us -> 147 us (0.961)
  Pallas kernels: 152 us -> 146 us
    pallas_call x1, Pallas kernels: 151 us -> 144 us  [run_step(): pl.pallas_call(step_kernel, out_shape=shapes, in_specs=[VM] * 13, out_spe...]
where the time goes in v2:
time: 147 us
  Pallas kernels  146 us (99%)
    pallas_call x1, Pallas kernels, run_step(): pl.pallas_call(step_kernel, out_shape=shapes, in_specs=[VM] * 13, out_spe...  144 us

profile of v2, /device:TPU:0, one launch (start us, length us, event | category | flops | bytes accessed | tf_op | source)
XLA Modules:
  0.0 146.6 jit_solution(8352501135762833142)
XLA Ops:
  0.6 144.3 %step.1 = (f32[12,768]{1,0:T(8,128)}, f32[12,768]{1,0:T(8,128)}, f32[13,768]{1,0:T(8,128)}, f32[4,768]{1,0:T(4,128)}, f32[8,128]{1,0:T(8,128)}) custom-call(bf16[26,2048]{1,0:T(8,128)(2,1)} %t_up.1, bf16[26,2048]{1,0:T(8,128)(2,1)} %t_down.1, bf16[12,768]{1,0:T(8,128)(2,1)} %bitcast.9, bf16[12,768]{1,0:T(8,128)(2,1)} %down.1, bf16[13,768]{1,0:T(8,128)(2,1)} %bitcast.10, ...), custom_call_target="tpu_custom_call" | custom-call | tf_op jit(solution)/shard_map/step/pallas_call | solution.py:750
  144.9 1.5 %write.1 = (f32[12,768]{1,0:T(8,128)}, f32[12,768]{1,0:T(8,128)}, f32[13,768]{1,0:T(8,128)}, f32[4,768]{1,0:T(4,128)}, f32[1,1]{1,0:T(1,128)}) custom-call(f32[12,768]{1,0:T(8,128)} %get-tuple-element.15.refs_0_, f32[12,768]{1,0:T(8,128)} %get-tuple-element.16.refs_1_, f32[13,768]{1,0:T(8,128)} %get-tuple-element.17.refs_2_, ...), custom_call_target="tpu_custom_call" | custom-call | tf_op jit(solution)/shard_map/write/pallas_call | solution.py:761

commit v3 on v2

--- a/solution.py
+++ b/solution.py
@@ -472,7 +472,7 @@
         chains["dD"[part]] = teacher(g_down, part, False)
         chains["eE"[part]] = teacher(g_down, part, True)
 
-    own_rows = gates.shape[0]
+    own_rows = normed.shape[0]
     own = pl.ds(pl.multiple_of(grp * own_rows, own_rows), own_rows)
     partner_rows = pl.ds(pl.multiple_of((1 - grp) * own_rows, own_rows), own_rows)
     step = 256
@@ -523,18 +523,18 @@
         out[y] = dot(t_act[rows, :], weights, 1, 1).astype(bf16)
 
     def ups(shape):
-        return iota(shape, 1) % (2 * hid) < hid
+        return iota(shape, 0) % (2 * hid) < hid
 
     def student(n):
         weights = g_pack[n // 4, n % 4].reshape(-1, g_pack.shape[-1])
         size = weights.shape[0]
-        cols = pl.ds(n * size, size)
-        gate = dot(normed[...], weights, 1, 1)
-        gates[:, cols] = gate
+        units = pl.ds(n * size, size)
+        gate = dot(weights, normed[...], 1, 1)
+        gates[units, :] = gate
         act = jnp.where(ups(gate.shape), gelu_tanh(gate), 0.0)
-        act = pltpu.roll(act, hid, 1).astype(bf16)
-        acts[:, cols] = act
-        part = dot(act, weights, 1, 0)
+        act = pltpu.roll(act, hid, 0).astype(bf16)
+        acts[units, :] = act
+        part = dot(act, weights, 0, 0)
         s_acc[...] = part + (s_in[own, :].astype(f32) if n == 0 else s_acc[...])
 
     def student_end():
@@ -665,11 +665,11 @@
     def pack_block(n, carry):
         weights = g_pack[n // 4, n % 4].reshape(-1, g_pack.shape[-1])
         size = weights.shape[0]
-        cols = pl.ds(pl.multiple_of(n * size, 128), size)
-        grad_act = pltpu.roll(dot(grad_out[...], weights, 1, 1), size - hid, 1)
-        grad_gate = jax.vjp(gelu_tanh, gates[:, cols])[1](grad_act)[0]
+        units = pl.ds(pl.multiple_of(n * size, 128), size)
+        grad_act = pltpu.roll(dot(weights, grad_out[...], 1, 1), size - hid, 0)
+        grad_gate = jax.vjp(gelu_tanh, gates[units, :])[1](grad_act)[0]
         grad_gate = jnp.where(ups(grad_gate.shape), grad_gate, 0.0).astype(bf16)
-        total = dot(grad_gate, normed[...], 0, 0) + dot(acts[:, cols], grad_out[...], 0, 0)
+        total = dot(grad_gate, normed[...], 1, 0) + dot(acts[units, :], grad_out[...], 1, 0)
         d_pack[n // 4, n % 4] = total.astype(bf16).reshape(d_pack.shape[2:])
         return carry
 
@@ -713,8 +713,8 @@
         vmem(whole + (2 * proj.shape[0], width // 2), bf16),
         vmem(tiles, f32),
         vmem(whole + (8, 128), f32),
-        vmem((own_rows, n_pack), f32),
-        vmem((own_rows, n_pack), bf16),
+        vmem((n_pack, own_rows), f32),
+        vmem((n_pack, own_rows), bf16),
         vmem((own_rows, width), bf16),
         vmem((own_rows, width), bf16),
         vmem((own_rows, n_wide), bf16),

time: 147 us -> 146 us (level)
  no operation moved by 1% of the time
where the time goes in v3:
time: 146 us
  Pallas kernels  145 us (99%)
    pallas_call x1, Pallas kernels, run_step(): pl.pallas_call(step_kernel, out_shape=shapes, in_specs=[VM] * 13, out_spe...  143 us

profile of v3, /device:TPU:0, one launch (start us, length us, event | category | flops | bytes accessed | tf_op | source)
XLA Modules:
  0.0 145.6 jit_solution(3865031243704600598)
XLA Ops:
  0.6 143.3 %step.1 = (f32[12,768]{1,0:T(8,128)}, f32[12,768]{1,0:T(8,128)}, f32[13,768]{1,0:T(8,128)}, f32[4,768]{1,0:T(4,128)}, f32[8,128]{1,0:T(8,128)}) custom-call(bf16[26,2048]{1,0:T(8,128)(2,1)} %t_up.1, bf16[26,2048]{1,0:T(8,128)(2,1)} %t_down.1, bf16[12,768]{1,0:T(8,128)(2,1)} %bitcast.9, bf16[12,768]{1,0:T(8,128)(2,1)} %down.1, bf16[13,768]{1,0:T(8,128)(2,1)} %bitcast.10, ...), custom_call_target="tpu_custom_call" | custom-call | tf_op jit(solution)/shard_map/step/pallas_call | solution.py:750
  143.9 1.5 %write.1 = (f32[12,768]{1,0:T(8,128)}, f32[12,768]{1,0:T(8,128)}, f32[13,768]{1,0:T(8,128)}, f32[4,768]{1,0:T(4,128)}, f32[1,1]{1,0:T(1,128)}) custom-call(f32[12,768]{1,0:T(8,128)} %get-tuple-element.15.refs_0_, f32[12,768]{1,0:T(8,128)} %get-tuple-element.16.refs_1_, f32[13,768]{1,0:T(8,128)} %get-tuple-element.17.refs_2_, ...), custom_call_target="tpu_custom_call" | custom-call | tf_op jit(solution)/shard_map/write/pallas_call | solution.py:761

commit v4 on v3

--- a/solution.py
+++ b/solution.py
@@ -675,8 +675,9 @@
 
     for part in range(4):
         lax.fori_loop(2 * part, 2 * part + 2, pack_block, 0)
-        for one in ends:
-            next(one, None)
+        if part % 2:
+            for one in ends:
+                next(one, None)
     pack_sums.push()
     ends.append(pack_sums.chain())
     for turn in range(8):

time: 146 us -> 142 us (0.973)
  Pallas kernels: 145 us -> 141 us
    pallas_call x1, Pallas kernels: 143 us -> 139 us  [run_step(): pl.pallas_call(step_kernel, out_shape=shapes, in_specs=[VM] * 13, out_spe...]
where the time goes in v4:
time: 142 us
  Pallas kernels  141 us (99%)
    pallas_call x1, Pallas kernels, run_step(): pl.pallas_call(step_kernel, out_shape=shapes, in_specs=[VM] * 13, out_spe...  139 us

profile of v4, /device:TPU:0, one launch (start us, length us, event | category | flops | bytes accessed | tf_op | source)
XLA Modules:
  0.0 141.7 jit_solution(578794931789569523)
XLA Ops:
  0.6 139.3 %step.1 = (f32[12,768]{1,0:T(8,128)}, f32[12,768]{1,0:T(8,128)}, f32[13,768]{1,0:T(8,128)}, f32[4,768]{1,0:T(4,128)}, f32[8,128]{1,0:T(8,128)}) custom-call(bf16[26,2048]{1,0:T(8,128)(2,1)} %t_up.1, bf16[26,2048]{1,0:T(8,128)(2,1)} %t_down.1, bf16[12,768]{1,0:T(8,128)(2,1)} %bitcast.9, bf16[12,768]{1,0:T(8,128)(2,1)} %down.1, bf16[13,768]{1,0:T(8,128)(2,1)} %bitcast.10, ...), custom_call_target="tpu_custom_call" | custom-call | tf_op jit(solution)/shard_map/step/pallas_call | solution.py:751
  140.0 1.5 %write.1 = (f32[12,768]{1,0:T(8,128)}, f32[12,768]{1,0:T(8,128)}, f32[13,768]{1,0:T(8,128)}, f32[4,768]{1,0:T(4,128)}, f32[1,1]{1,0:T(1,128)}) custom-call(f32[12,768]{1,0:T(8,128)} %get-tuple-element.15.refs_0_, f32[12,768]{1,0:T(8,128)} %get-tuple-element.16.refs_1_, f32[13,768]{1,0:T(8,128)} %get-tuple-element.17.refs_2_, ...), custom_call_target="tpu_custom_call" | custom-call | tf_op jit(solution)/shard_map/write/pallas_call | solution.py:762
